TPU v7x, 32 devices: a whole 2x2x4 slice. The times are simulated.
32 devices in a mesh: dp: 16 (over z, y, x), rep: 2 (over core).
Axes of the slice: x: 2, y: 2, z: 4, core: 2. Of those that a mesh axis runs over, the one named last changes fastest.
Arguments:
- ids: int32 [8192], P(('dp', 'rep')), may hold values from 0 to 65520
- counts: int32 [32], P(('dp', 'rep')), may hold values from 1 to 256, as said below
- hash_scale: int32 [512], replicated, may hold values from 1 to 32767
- hash_shift: int32 [512], replicated, may hold values from 0 to 65520
- w_code: bfloat16 [512, 1024], replicated, may hold values from -0.25 to 0.25
- norm_gain: float32 [1024], replicated, may hold values from 0.5 to 1.5
- norm_bias: float32 [1024], replicated, may hold values from -3 to 3
- w_out: bfloat16 [1024, 128], replicated, may hold values from -0.1875 to 0.1875
- out_bias: float32 [128], replicated, may hold values from -3 to 3
- cotangent: bfloat16 [8192, 128], P(('dp', 'rep')), may hold values from -6 to 6
Outputs:
- embeddings: bfloat16 [8192, 128], P(('dp', 'rep'))
- grad_code_t: float32 [1024, 512], P(('dp', 'rep'))
- grad_out: float32 [1024, 128], P(('dp', 'rep'))
- grad_gain: float32 [1024], replicated
- grad_bias: float32 [1024], replicated
Inputs may be any that keep to these rules, and one draw needn't show every extreme that they name: Each device has 1 to 256 live slots, the first ones of its slots; the counts of the devices of one rep index sum to exactly 1024, and in each such group one device has exactly 256.
All inputs are finite; a program needn't handle non-finite values.
Results may differ from a plain program's by a relative error of at most 0.006.
Values may be sent and summed in bfloat16 or wider, within the bound.
No kernel may reach another device: no remote copies, remote signals or barrier semaphores. Data moves between devices by JAX's collectives and lax.ppermute only.
A program may use at most 64 MiB of HBM per device.

v0:
```python
import math
import jax
import jax.numpy as jnp
from jax import lax
from jax.sharding import PartitionSpec as P

BLOCK = 256
modulus = 65521
epsilon = 1e-05


def hashed(ident, hash_scale, hash_shift):
    resid = ident % modulus
    bucket = (hash_scale[None, :] * resid[:, None] + hash_shift[None, :]) % modulus
    return (bucket.astype(jnp.float32) * (2.0 / (modulus - 1)) - 1.0).astype(jnp.bfloat16)


def mish_parts(gated):
    softer = jax.nn.softplus(gated)
    tangent = jnp.tanh(softer)
    return (gated * tangent, tangent + gated * (1.0 - tangent * tangent) * jax.nn.sigmoid(gated))


def owner_rows(dpre_rows, row_ids, hash_scale, hash_shift):
    dp_count = lax.axis_size("dp")
    rep_count = lax.axis_size("rep")
    device_count = dp_count * rep_count
    row_count = dpre_rows.shape[0]
    columns = lax.all_to_all(
        lax.all_to_all(dpre_rows, "dp", split_axis=1, concat_axis=0, tiled=True),
        "rep",
        split_axis=1,
        concat_axis=0,
        tiled=True,
    )
    everyone = lax.all_gather(row_ids, ("dp", "rep"), axis=0, tiled=True)
    everyone = everyone.reshape(dp_count, rep_count, row_count).transpose(1, 0, 2).reshape(-1)
    group = math.gcd(device_count, max(1, 8192 // row_count))
    step_rows = group * row_count

    def accumulate(index, grad_rows):
        start = index * step_rows
        id_block = lax.dynamic_slice_in_dim(everyone, start, step_rows, 0)
        col_block = lax.dynamic_slice_in_dim(columns, start, step_rows, 0)
        code_block = hashed(id_block, hash_scale, hash_shift)
        return grad_rows + lax.dot_general(
            col_block, code_block, (((0,), (0,)), ((), ())), preferred_element_type=jnp.float32
        )

    start_rows = jnp.zeros((columns.shape[1], hash_scale.shape[0]), jnp.float32)
    return lax.fori_loop(0, device_count // group, accumulate, start_rows)


def train_rows(
    code_rows,
    cot_rows,
    live_count,
    row_ids,
    hash_scale,
    hash_shift,
    w_code,
    norm_gain,
    norm_bias,
    w_out,
    out_bias,
):
    row_count = code_rows.shape[0]
    hidden = w_code.shape[1]
    width = w_out.shape[1]
    live_flags = jnp.arange(row_count, dtype=jnp.int32) < live_count
    block_total = (live_count + BLOCK - 1) // BLOCK
    zero_row = jnp.zeros((hidden,), jnp.float32)

    def first_pass(block_index, state_carry):
        stored, sum_hidden, sum_square = state_carry
        keep_rows = live_flags[:, None]
        preact = jnp.dot(code_rows, w_code, preferred_element_type=jnp.float32)
        masked = jnp.where(keep_rows, preact, 0.0)
        stored = preact
        return (stored, sum_hidden + masked.sum(0), sum_square + (masked * masked).sum(0))

    stored, sum_hidden, sum_square = lax.fori_loop(
        0,
        block_total,
        first_pass,
        (jnp.zeros((row_count, hidden), jnp.float32), zero_row, zero_row),
    )
    sum_hidden, sum_square, total = lax.psum(
        (sum_hidden, sum_square, live_count.astype(jnp.float32)), ("dp", "rep")
    )
    feature_mean = sum_hidden / total
    inv_std = lax.rsqrt(sum_square / total - feature_mean * feature_mean + epsilon)
    loss_scale = lax.rsqrt(total)

    def second_pass(block_index, state_carry):
        stored, dvalue_rows, embedded, grad_gain, grad_bias, grad_out = state_carry
        keep_rows = live_flags[:, None]
        normed = (stored - feature_mean) * inv_std
        act_full, mish_slope = mish_parts(normed * norm_gain + norm_bias)
        activation = act_full.astype(jnp.bfloat16)
        out_rows = jnp.dot(activation, w_out, preferred_element_type=jnp.float32) + out_bias
        out_rows = jnp.where(keep_rows, out_rows, 0.0).astype(jnp.bfloat16)
        delta_rows = jnp.where(keep_rows, cot_rows.astype(jnp.float32) * loss_scale, 0.0).astype(
            jnp.bfloat16
        )
        grad_act = lax.dot_general(
            delta_rows, w_out, (((1,), (1,)), ((), ())), preferred_element_type=jnp.float32
        )
        dvalue = grad_act * mish_slope
        stored = normed
        dvalue_rows = dvalue
        embedded = out_rows
        out_part = lax.dot_general(
            activation, delta_rows, (((0,), (0,)), ((), ())), preferred_element_type=jnp.float32
        )
        return (
            stored,
            dvalue_rows,
            embedded,
            grad_gain + (dvalue * normed).sum(0),
            grad_bias + dvalue.sum(0),
            grad_out + out_part,
        )

    start_state = (
        stored,
        jnp.zeros((row_count, hidden), jnp.float32),
        jnp.zeros((row_count, width), jnp.bfloat16),
        zero_row,
        zero_row,
        jnp.zeros((hidden, width), jnp.float32),
    )
    stored, dvalue_rows, embedded, grad_gain, grad_bias, grad_out = lax.fori_loop(
        0, block_total, second_pass, start_state
    )
    grad_gain, grad_bias = lax.psum((grad_gain, grad_bias), ("dp", "rep"))

    def signal_block():
        keep_rows = live_flags[:, None]
        dpre = norm_gain * inv_std * (dvalue_rows - grad_bias / total - stored * grad_gain / total)
        return jnp.where(keep_rows, dpre, 0.0).astype(jnp.bfloat16)

    def store_pass(block_index, dpre_rows):
        return signal_block()

    dpre_rows = lax.fori_loop(
        0, block_total, store_pass, jnp.zeros((row_count, hidden), jnp.bfloat16)
    )
    out_share = lax.psum_scatter(grad_out, ("dp", "rep"), scatter_dimension=0, tiled=True)
    code_share = owner_rows(dpre_rows, row_ids, hash_scale, hash_shift)
    return (embedded, code_share, out_share, grad_gain, grad_bias)


def per_device(
    ids, counts, hash_scale, hash_shift, w_code, norm_gain, norm_bias, w_out, out_bias, cotangent
):
    live_count = counts[0]
    weights = (w_code, norm_gain, norm_bias, w_out, out_bias)
    code_rows = hashed(ids, hash_scale, hash_shift)
    embedded, code_share, out_share, grad_gain, grad_bias = train_rows(
        code_rows, cotangent, live_count, ids, hash_scale, hash_shift, *weights
    )
    return (embedded, code_share, out_share, grad_gain, grad_bias)


def solution(mesh):
    return jax.shard_map(
        per_device,
        mesh=mesh,
        in_specs=(
            P(("dp", "rep")),
            P(("dp", "rep")),
            P(),
            P(),
            P(),
            P(),
            P(),
            P(),
            P(),
            P(("dp", "rep"), None),
        ),
        out_specs=(
            P(("dp", "rep"), None),
            P(("dp", "rep"), None),
            P(("dp", "rep"), None),
            P(),
            P(),
        ),
        check_vma=False,
    )
```

profile of v0, /device:TPU:0, one launch (start us, length us, event | category | flops | bytes accessed | tf_op | source)
XLA Modules:
  0.0 264.1 jit_solution(4582363690425462505)
XLA Ops:
  7.9 0.7 and_select_fusion
  8.6 1.4 multiply_reduce_fusion.1
  10.1 1.1 broadcast.69.clone
  11.2 1.0 while.57
  11.2 1.0 copy.38
  12.3 42.2 %all-reduce.1 = (f32[1024]{0:T(1024)S(1)}, f32[]{:T(128)}, f32[1024]{0:T(1024)S(1)}) all-reduce(f32[1024]{0:T(1024)S(1)} %get-tuple-element.387, f32[]{:T(128)S(6)} %convert_element_type.36, f32[1024]{0:T(1024)S(1)} %get-tuple-element.388), channel_id=1, replica_groups=mesh['dp'=16,'rep'=2] {'dp','rep'}, use_global_device_ids=true, to_apply=%region_4.5 | all-reduce | flops 2049 | bytes 16392 | tf_op jit(solution)/shard_map/psum | solution.py:88
  55.2 0.7 fusion.43
  55.8 1.1 broadcast.69
  57.0 0.6 broadcast_in_dim.81
  57.6 5.0 %while.58 = (s32[]{:T(128)}, f32[256,1024]{1,0:T(8,128)S(1)}, f32[256,1024]{1,0:T(8,128)}, bf16[256,128]{1,0:T(8,128)(2,1)}, f32[1024]{0:T(1024)S(1)}, /*index=5...) while((s32[]{:T(128)}, f32[256,1024]{1,0:T(8,128)S(1)}, ...), condition=%wide.region_10.11_spmd.clone, body=%wide.region_7.10_spmd.clone.sunk | while | flops 210206976 | bytes 7595697 | solution.py:133
  57.7 0.8 multiply_convert_fusion.2
  58.4 0.7 iota_compare_fusion.5
  59.1 2.2 fusion.60
  61.3 0.4 convolution_add_fusion.3
  61.7 0.9 fusion.61
  62.7 40.3 %all-reduce = (f32[1024]{0:T(1024)S(1)}, f32[1024]{0:T(1024)S(1)}) all-reduce(f32[1024]{0:T(1024)S(1)} %get-tuple-element.390, f32[1024]{0:T(1024)S(1)} %get-tuple-element.392), channel_id=1, replica_groups=mesh['dp'=16,'rep'=2] {'dp','rep'}, use_global_device_ids=true, to_apply=%region_11.12 | all-reduce | flops 2048 | bytes 16384 | tf_op jit(solution)/shard_map/psum | solution.py:136
  103.0 0.8 broadcast_in_dim.83
  103.9 4.2 %while.59 = (s32[]{:T(128)}, bf16[256,1024]{1,0:T(8,128)(2,1)}, s32[]{:T(128)}, f32[1,1024]{1,0:T(1,128)S(1)}, f32[]{:T(128)}, /*index=5*/f32[1024]{0:T(1024)S(1...) while((s32[]{:T(128)}, bf16[256,1024]{1,0:T(8,128)(2,1)}, ...), condition=%wide.region_14.15_spmd.clone, body=%wide.region_13.14_spmd.clone.sunk | while | flops 1836290 | bytes 2642553 | solution.py:146
  103.9 0.6 broadcast_divide_fusion.3
  104.5 0.7 iota_compare_fusion.6
  105.2 2.9 %select_convert_fusion.7 = bf16[256,1024]{1,0:T(8,128)(2,1)} fusion(f32[256,1024]{1,0:T(8,128)S(1)} %get-tuple-element.870, f32[256,1024]{1,0:T(8,128)} %get-tuple-element.868, f32[]{:T(128)} %get-tuple-element.866, f32[1024]{0:T(1024)S(1)} %get-tuple-element.869, f32[1024]{0:T(1024)S(1)} %broadcast_divide_fusion.3, f32[1024]{0:T(1024)S(1)} %bitcast.37, ...), kind=kLoop, calls=%fused_computation.18.clone.1 | loop fusion | flops 1835008 | bytes 2633988 | tf_op jit(solution)/shard_map/while/body/convert_element_type | solution.py:141
  108.1 2.0 copy.22
  110.1 6.4 %all-to-all-start = ((bf16[256,16,64]{0,2,1:T(8,128)(2,1)}), bf16[256,16,64]{0,2,1:T(8,128)(2,1)S(1)}, u32[]{:S(2)}, u32[]{:S(2)}) async-start(bf16[256,16,64]{0,2,1:T(8,128)(2,1)} %bitcast.2), calls=%async_computation | async-start | bytes 1048576 | tf_op jit(solution)/shard_map/all_to_all | solution.py:30
  116.5 0.0 reduce-scatter.2.cloned.1.call-start
  116.6 0.7 reduce-scatter.2.cloned.1.call-update
  117.3 41.9 %all-gather = s32[32,1,256]{2,1,0:T(1,128)S(1)} all-gather(s32[1,1,256]{2,1,0:T(1,128)S(1)} %bitcast.41), channel_id=1, replica_groups=mesh['dp'=16,'rep'=2] {'dp','rep'}, dimensions={0}, use_global_device_ids=true | all-gather | bytes 33792 | tf_op jit(solution)/shard_map/all_gather | solution.py:36
  159.2 0.2 remainder_reduce_fusion
  159.4 0.3 copy.23
  159.7 0.2 all_to_all.29
  160.0 4.2 %all_to_all.35 = bf16[4096,2,32]{0,2,1:T(8,128)(2,1)S(1)} all-to-all(bf16[4096,2,32]{0,2,1:T(8,128)(2,1)S(1)} %all_to_all.29), channel_id=1, replica_groups=mesh['dp'=16,'rep'=2] {'rep'}, dimensions={1} | all-to-all | bytes 1048576 | tf_op jit(solution)/shard_map/all_to_all | solution.py:29
  164.2 11.9 %fusion.16 = f32[32,512]{1,0:T(8,128)} fusion(bf16[8192,32]{0,1:T(8,128)(2,1)S(1)} %bitcast.35, s32[512]{0:T(512)S(1)} %copy-done.11, s32[8192]{0:T(1024)S(1)} %add_select_fusion.2, s32[512]{0:T(512)S(1)} %copy-done.12), kind=kOutput, calls=%fused_computation.30 | convolution fusion | flops 318767104 | bytes 626688 | tf_op jit(solution)/shard_map/while/body/eval_jaxpr/dot_general | solution.py:46
  176.1 81.1 %reduce-scatter.2.cloned.1.call-done = f32[32,128]{1,0:T(8,128)} async-done(((f32[1024,128]{1,0:T(8,128)}), f32[32,128]{1,0:T(8,128)}) %reduce-scatter.2.cloned.1.call-update) | async-done | bytes 16400 | tf_op jit(solution)/shard_map/reduce_scatter | solution.py:149
  (42 shorter events, 0.2 us)
Async XLA Ops:
  7.2 1.5 copy-start
  11.2 43.9 %copy-start.5 = (f32[1024]{0:T(1024)S(1)}, f32[1024]{0:T(1024)}, u32[]{:S(2)}) copy-start(f32[1024]{0:T(1024)} %param.21) | copy-start | bytes 12292
  12.2 45.4 %copy-start.1 = (f32[256,1024]{1,0:T(8,128)S(1)}, f32[256,1024]{1,0:T(8,128)}, u32[]{:S(2)}) copy-start(f32[256,1024]{1,0:T(8,128)} %get-tuple-element.787) | copy-start | bytes 3145732
  12.2 45.4 %copy-start.3 = (bf16[1024,128]{1,0:T(8,128)(2,1)S(1)}, bf16[1024,128]{1,0:T(8,128)(2,1)}, u32[]{:S(2)}) copy-start(bf16[1024,128]{1,0:T(8,128)(2,1)} %param.23) | copy-start | bytes 786436
  12.3 45.3 %copy-start.4 = (bf16[256,128]{1,0:T(8,128)(2,1)S(1)}, bf16[256,128]{1,0:T(8,128)(2,1)}, u32[]{:S(2)}) copy-start(bf16[256,128]{1,0:T(8,128)(2,1)} %param.25) | copy-start | bytes 196612
  12.3 45.3 %copy-start.6 = (f32[1024]{0:T(1024)S(1)}, f32[1024]{0:T(1024)}, u32[]{:S(2)}) copy-start(f32[1024]{0:T(1024)} %param.22) | copy-start | bytes 12292
  12.3 45.3 %copy-start.9 = (f32[128]{0:T(128)S(1)}, f32[128]{0:T(128)}, u32[]{:S(2)}) copy-start(f32[128]{0:T(128)} %param.24) | copy-start | bytes 1540
  62.7 41.2 %copy-start.2 = (f32[1024,128]{1,0:T(8,128)}, f32[1024,128]{1,0:T(8,128)S(1)}, u32[]{:S(2)}) copy-start(f32[1024,128]{1,0:T(8,128)S(1)} %get-tuple-element.395) | copy-start | bytes 1572868
  108.1 2.0 copy-start.7
  108.1 2.1 copy-start.8
  110.1 7.1 %copy-start.10 = (s32[256]{0:T(256)S(1)}, s32[256]{0:T(256)}, u32[]{:S(2)}) copy-start(s32[256]{0:T(256)} %param.16) | copy-start | bytes 3076
  110.1 49.3 %all-to-all-start = ((bf16[256,16,64]{0,2,1:T(8,128)(2,1)}), bf16[256,16,64]{0,2,1:T(8,128)(2,1)S(1)}, u32[]{:S(2)}, u32[]{:S(2)}) async-start(bf16[256,16,64]{0,2,1:T(8,128)(2,1)} %bitcast.2), calls=%async_computation | async-start | bytes 1048576 | tf_op jit(solution)/shard_map/all_to_all | solution.py:30
  116.5 140.7 %reduce-scatter.2.cloned.1.call-start = ((), (), s32[]{:S(2)}) async-start(), calls=%async_computation.3 | async-start | bytes 540672 | tf_op jit(solution)/shard_map/reduce_scatter | solution.py:149
  160.0 4.2 %copy-start.11 = (s32[512]{0:T(512)S(1)}, s32[512]{0:T(512)}, u32[]{:S(2)}) copy-start(s32[512]{0:T(512)} %param.19) | copy-start | bytes 6148
  160.0 4.2 %copy-start.12 = (s32[512]{0:T(512)S(1)}, s32[512]{0:T(512)}, u32[]{:S(2)}) copy-start(s32[512]{0:T(512)} %param.18) | copy-start | bytes 6148
Sparse Core Ops, SparseCore 0:
  120.1 137.0 reduce-scatter.1
where the time goes:
time: 265 us; the launch traced here: 264 us
  blocking collectives  129 us (49%)
  waiting for transfers between devices  81.8 us (31%)
  matrix products  16.9 us (6%)
  between operations  15.7 us (6%)
  local copies, waits for them, and re-layouts  7.5 us (3%)
  other arithmetic  7.18 us (3%)
  starting transfers between devices  6.41 us (2%)
    reduce_scatter x1, waiting for transfers between devices, train_rows(): lax.psum_scatter(grad_out, ('dp', 'rep'), scatter_dimension=0, tiled=True)  81.1 us
    psum x1, blocking collectives, train_rows(): lax.psum((sum_hidden, sum_square, live_count.astype(jnp.float32)), ('dp',...  42.2 us
    all_gather x1, blocking collectives, owner_rows(): everyone = lax.all_gather(row_ids, ('dp', 'rep'), axis=0, tiled=True)  41.9 us
    psum x1, blocking collectives, train_rows(): grad_gain, grad_bias = lax.psum((grad_gain, grad_bias), ('dp', 'rep'))  40.3 us
    dot_general x1, matrix products, accumulate(): lax.dot_general(col_block, code_block, (((0,), (0,)), ((), ())), preferre...  11.9 us
    all_to_all x1, starting transfers between devices, owner_rows(): lax.all_to_all(dpre_rows, 'dp', split_axis=1, concat_axis=0, tiled=True)  6.37 us
  transfers between devices with their start and end apart: 2, of which 1 were waited for; matrix products, arithmetic and copies ran while one was open for 5% of the time, Pallas kernels for 0%

commit v1 on v0

--- a/solution.py
+++ b/solution.py
@@ -133,7 +133,7 @@
     stored, dvalue_rows, embedded, grad_gain, grad_bias, grad_out = lax.fori_loop(
         0, block_total, second_pass, start_state
     )
-    grad_gain, grad_bias = lax.psum((grad_gain, grad_bias), ("dp", "rep"))
+    grad_gain, grad_bias = lax.psum(lax.psum((grad_gain, grad_bias), "rep"), "dp")
 
     def signal_block():
         keep_rows = live_flags[:, None]

time: 265 us -> 265 us (level)
  blocking collectives: 129 us -> 132 us
  starting transfers between devices: 6.41 us -> 3.75 us
    psum x1 -> x2, blocking collectives: 40.3 us -> 43.6 us  [the longest x1 41.1 us: train_rows(): lax.psum(lax.psum((grad_gain, grad_bias), 'rep'), 'dp')]
    all_to_all x1, starting transfers between devices: 6.37 us -> 3.71 us  [owner_rows(): lax.all_to_all(dpre_rows, 'dp', split_axis=1, concat_axis=0, tiled=True)]
where the time goes in v1:
time: 265 us
  blocking collectives  132 us (50%)
  waiting for transfers between devices  81.8 us (31%)
  matrix products  16.9 us (6%)
  between operations  15.7 us (6%)
  local copies, waits for them, and re-layouts  7.54 us (3%)
  other arithmetic  7.19 us (3%)
  starting transfers between devices  3.75 us (1%)
    reduce_scatter x1, waiting for transfers between devices, train_rows(): lax.psum_scatter(grad_out, ('dp', 'rep'), scatter_dimension=0, tiled=True)  81.1 us
    psum x1, blocking collectives, train_rows(): lax.psum((sum_hidden, sum_square, live_count.astype(jnp.float32)), ('dp',...  42.2 us
    all_gather x1, blocking collectives, owner_rows(): everyone = lax.all_gather(row_ids, ('dp', 'rep'), axis=0, tiled=True)  41.9 us
    psum x1, blocking collectives, train_rows(): lax.psum(lax.psum((grad_gain, grad_bias), 'rep'), 'dp')  41.1 us
    dot_general x1, matrix products, accumulate(): lax.dot_general(col_block, code_block, (((0,), (0,)), ((), ())), preferre...  11.9 us
  transfers between devices with their start and end apart: 2, of which 1 were waited for; matrix products, arithmetic and copies ran while one was open for 5% of the time, Pallas kernels for 0%

profile of v1, /device:TPU:0, one launch (start us, length us, event | category | flops | bytes accessed | tf_op | source)
XLA Modules:
  0.0 264.8 jit_solution(12155949675315968485)
XLA Ops:
  7.9 0.7 and_select_fusion
  8.6 1.4 multiply_reduce_fusion.1
  10.1 1.1 broadcast.69.clone
  11.2 1.0 while.57
  11.2 1.0 copy.38
  12.3 42.2 %all-reduce = (f32[1024]{0:T(1024)S(1)}, f32[]{:T(128)}, f32[1024]{0:T(1024)S(1)}) all-reduce(f32[1024]{0:T(1024)S(1)} %get-tuple-element.387, f32[]{:T(128)S(6)} %convert_element_type.36, f32[1024]{0:T(1024)S(1)} %get-tuple-element.388), channel_id=1, replica_groups=mesh['dp'=16,'rep'=2] {'dp','rep'}, use_global_device_ids=true, to_apply=%region_4.5 | all-reduce | flops 2049 | bytes 16392 | tf_op jit(solution)/shard_map/psum | solution.py:88
  55.2 0.7 fusion.43
  55.9 1.1 broadcast.69
  57.0 0.6 broadcast_in_dim.81
  57.7 5.0 %while.58 = (s32[]{:T(128)}, f32[256,1024]{1,0:T(8,128)S(1)}, f32[256,1024]{1,0:T(8,128)}, bf16[256,128]{1,0:T(8,128)(2,1)}, f32[1024]{0:T(1024)S(1)}, /*index=5...) while((s32[]{:T(128)}, f32[256,1024]{1,0:T(8,128)S(1)}, ...), condition=%wide.region_10.11_spmd.clone, body=%wide.region_7.10_spmd.clone.sunk | while | flops 210206976 | bytes 7595697 | solution.py:133
  57.7 0.8 multiply_convert_fusion.2
  58.5 0.7 iota_compare_fusion.5
  59.1 2.2 fusion.60
  61.4 0.4 convolution_add_fusion.3
  61.8 0.9 fusion.61
  62.7 2.5 all-reduce.2
  65.2 41.1 %all-reduce.1 = (f32[1024]{0:T(1024)S(1)}, f32[1024]{0:T(1024)S(1)}) all-reduce(f32[1024]{0:T(1024)S(1)} %get-tuple-element.534, f32[1024]{0:T(1024)S(1)} %get-tuple-element.535), channel_id=1, replica_groups=mesh['dp'=16,'rep'=2] {'dp'}, use_global_device_ids=true, to_apply=%region_12.13 | all-reduce | flops 2048 | bytes 16384 | tf_op jit(solution)/shard_map/psum | solution.py:136
  106.3 0.9 broadcast_in_dim.83
  107.2 4.2 %while.59 = (s32[]{:T(128)}, bf16[256,1024]{1,0:T(8,128)(2,1)}, s32[]{:T(128)}, f32[1,1024]{1,0:T(1,128)S(1)}, f32[]{:T(128)}, /*index=5*/f32[1024]{0:T(1024)S(1...) while((s32[]{:T(128)}, bf16[256,1024]{1,0:T(8,128)(2,1)}, ...), condition=%wide.region_16.17_spmd.clone, body=%wide.region_15.16_spmd.clone.sunk | while | flops 1836290 | bytes 2642553 | solution.py:146
  107.2 0.6 broadcast_divide_fusion.3
  107.9 0.7 iota_compare_fusion.6
  108.5 2.9 %select_convert_fusion.7 = bf16[256,1024]{1,0:T(8,128)(2,1)} fusion(f32[256,1024]{1,0:T(8,128)S(1)} %get-tuple-element.872, f32[256,1024]{1,0:T(8,128)} %get-tuple-element.870, f32[]{:T(128)} %get-tuple-element.868, f32[1024]{0:T(1024)S(1)} %get-tuple-element.871, f32[1024]{0:T(1024)S(1)} %broadcast_divide_fusion.3, f32[1024]{0:T(1024)S(1)} %bitcast.37, ...), kind=kLoop, calls=%fused_computation.18.clone.1 | loop fusion | flops 1835008 | bytes 2633988 | tf_op jit(solution)/shard_map/while/body/convert_element_type | solution.py:141
  111.5 2.0 copy.22
  113.5 3.7 %all-to-all-start = ((bf16[256,16,64]{0,2,1:T(8,128)(2,1)}), bf16[256,16,64]{0,2,1:T(8,128)(2,1)S(1)}, u32[]{:S(2)}, u32[]{:S(2)}) async-start(bf16[256,16,64]{0,2,1:T(8,128)(2,1)} %bitcast.2), calls=%async_computation | async-start | bytes 1048576 | tf_op jit(solution)/shard_map/all_to_all | solution.py:30
  117.3 0.7 reduce-scatter.2.cloned.1.call-update
  118.0 41.9 %all-gather = s32[32,1,256]{2,1,0:T(1,128)S(1)} all-gather(s32[1,1,256]{2,1,0:T(1,128)S(1)} %bitcast.41), channel_id=1, replica_groups=mesh['dp'=16,'rep'=2] {'dp','rep'}, dimensions={0}, use_global_device_ids=true | all-gather | bytes 33792 | tf_op jit(solution)/shard_map/all_gather | solution.py:36
  159.8 0.2 remainder_reduce_fusion
  160.1 0.3 copy.23
  160.4 0.2 all_to_all.29
  160.7 4.2 %all_to_all.35 = bf16[4096,2,32]{0,2,1:T(8,128)(2,1)S(1)} all-to-all(bf16[4096,2,32]{0,2,1:T(8,128)(2,1)S(1)} %all_to_all.29), channel_id=1, replica_groups=mesh['dp'=16,'rep'=2] {'rep'}, dimensions={1} | all-to-all | bytes 1048576 | tf_op jit(solution)/shard_map/all_to_all | solution.py:29
  164.9 11.9 %fusion.16 = f32[32,512]{1,0:T(8,128)} fusion(bf16[8192,32]{0,1:T(8,128)(2,1)S(1)} %bitcast.35, s32[512]{0:T(512)S(1)} %copy-done.11, s32[8192]{0:T(1024)S(1)} %add_select_fusion.2, s32[512]{0:T(512)S(1)} %copy-done.12), kind=kOutput, calls=%fused_computation.30 | convolution fusion | flops 318767104 | bytes 626688 | tf_op jit(solution)/shard_map/while/body/eval_jaxpr/dot_general | solution.py:46
  176.8 81.1 %reduce-scatter.2.cloned.1.call-done = f32[32,128]{1,0:T(8,128)} async-done(((f32[1024,128]{1,0:T(8,128)}), f32[32,128]{1,0:T(8,128)}) %reduce-scatter.2.cloned.1.call-update) | async-done | bytes 16400 | tf_op jit(solution)/shard_map/reduce_scatter | solution.py:149
  (43 shorter events, 0.3 us)
Async XLA Ops:
  7.2 1.5 copy-start
  11.2 44.0 %copy-start.5 = (f32[1024]{0:T(1024)S(1)}, f32[1024]{0:T(1024)}, u32[]{:S(2)}) copy-start(f32[1024]{0:T(1024)} %param.21) | copy-start | bytes 12292
  12.3 45.4 %copy-start.1 = (f32[256,1024]{1,0:T(8,128)S(1)}, f32[256,1024]{1,0:T(8,128)}, u32[]{:S(2)}) copy-start(f32[256,1024]{1,0:T(8,128)} %get-tuple-element.789) | copy-start | bytes 3145732
  12.3 45.4 %copy-start.3 = (bf16[1024,128]{1,0:T(8,128)(2,1)S(1)}, bf16[1024,128]{1,0:T(8,128)(2,1)}, u32[]{:S(2)}) copy-start(bf16[1024,128]{1,0:T(8,128)(2,1)} %param.23) | copy-start | bytes 786436
  12.3 45.4 %copy-start.4 = (bf16[256,128]{1,0:T(8,128)(2,1)S(1)}, bf16[256,128]{1,0:T(8,128)(2,1)}, u32[]{:S(2)}) copy-start(bf16[256,128]{1,0:T(8,128)(2,1)} %param.25) | copy-start | bytes 196612
  12.3 45.4 %copy-start.6 = (f32[1024]{0:T(1024)S(1)}, f32[1024]{0:T(1024)}, u32[]{:S(2)}) copy-start(f32[1024]{0:T(1024)} %param.22) | copy-start | bytes 12292
  12.3 45.4 %copy-start.9 = (f32[128]{0:T(128)S(1)}, f32[128]{0:T(128)}, u32[]{:S(2)}) copy-start(f32[128]{0:T(128)} %param.24) | copy-start | bytes 1540
  62.7 44.5 %copy-start.2 = (f32[1024,128]{1,0:T(8,128)}, f32[1024,128]{1,0:T(8,128)S(1)}, u32[]{:S(2)}) copy-start(f32[1024,128]{1,0:T(8,128)S(1)} %get-tuple-element.395) | copy-start | bytes 1572868
  111.4 2.0 copy-start.7
  111.4 2.0 copy-start.8
  113.5 4.5 %copy-start.10 = (s32[256]{0:T(256)S(1)}, s32[256]{0:T(256)}, u32[]{:S(2)}) copy-start(s32[256]{0:T(256)} %param.16) | copy-start | bytes 3076
  113.5 46.6 %all-to-all-start = ((bf16[256,16,64]{0,2,1:T(8,128)(2,1)}), bf16[256,16,64]{0,2,1:T(8,128)(2,1)S(1)}, u32[]{:S(2)}, u32[]{:S(2)}) async-start(bf16[256,16,64]{0,2,1:T(8,128)(2,1)} %bitcast.2), calls=%async_computation | async-start | bytes 1048576 | tf_op jit(solution)/shard_map/all_to_all | solution.py:30
  117.2 140.7 %reduce-scatter.2.cloned.1.call-start = ((), (), s32[]{:S(2)}) async-start(), calls=%async_computation.3 | async-start | bytes 540672 | tf_op jit(solution)/shard_map/reduce_scatter | solution.py:149
  160.6 4.2 %copy-start.11 = (s32[512]{0:T(512)S(1)}, s32[512]{0:T(512)}, u32[]{:S(2)}) copy-start(s32[512]{0:T(512)} %param.19) | copy-start | bytes 6148
  160.6 4.2 %copy-start.12 = (s32[512]{0:T(512)S(1)}, s32[512]{0:T(512)}, u32[]{:S(2)}) copy-start(s32[512]{0:T(512)} %param.18) | copy-start | bytes 6148
Sparse Core Ops, SparseCore 0:
  120.8 137.0 reduce-scatter.1
